TPU v7x, 32 devices: a whole 2x2x4 slice. The times are simulated.
32 devices in a mesh: rows: 8 (over z, y), model: 4 (over x, core).
Axes of the slice: x: 2, y: 2, z: 4, core: 2. Of those that a mesh axis runs over, the one named last changes fastest.
Arguments:
- w_query: float32 [4096, 4096], P('rows', 'model'), may hold values from -0.125 to 0.125
- first_query: float32 [4096, 4096], P('rows', 'model'), may hold values from -6 to 6
- second_query: float32 [4096, 4096], P('rows', 'model'), may hold values from 0.1 to 10
- w_key: float32 [4096, 1024], P('rows', 'model'), may hold values from -0.125 to 0.125
- first_key: float32 [4096, 1024], P('rows', 'model'), may hold values from -6 to 6
- second_key: float32 [4096, 1024], P('rows', 'model'), may hold values from 0.1 to 10
- w_value: float32 [4096, 1024], P('rows', 'model'), may hold values from -0.125 to 0.125
- first_value: float32 [4096, 1024], P('rows', 'model'), may hold values from -6 to 6
- second_value: float32 [4096, 1024], P('rows', 'model'), may hold values from 0.1 to 10
- norm_train: float32 [4096], P(('rows', 'model')), may hold values from 0.25 to 1.75
- norm_step: float32 [4096], P(('rows', 'model')), may hold values from -0.3 to 0.3
Outputs:
- final_query: bfloat16 [4096, 4096], P(None, 'model')
- final_key: bfloat16 [4096, 1024], P(None, 'model')
- final_value: bfloat16 [4096, 1024], P(None, 'model')
- column_query: float32 [4096], P('model')
- column_key: float32 [1024], P('model')
- column_value: float32 [1024], P('model')
- serve_norm: bfloat16 [4096], replicated
- result_query: float32 [4096, 4096], P('rows', 'model')
- result_key: float32 [4096, 1024], P('rows', 'model')
- result_value: float32 [4096, 1024], P('rows', 'model')
All inputs are finite; a program needn't handle non-finite values. Where the computation divides by a largest or mean magnitude, that divisor is 1e-20 or more.
Results may differ from a plain program's by a relative error of at most 0.0004.
Values may be sent and summed in bfloat16 or wider, within the bound.
A program may use at most 64 MiB of HBM per device.

v0:
```python
import jax
import jax.numpy as jnp
from jax import lax
from jax.sharding import PartitionSpec as P

D_MODEL = 4096


learn_rate = 0.01
decay_rate = 0.05
tiny_value = 1e-08


def body(
    w_query,
    first_query,
    second_query,
    w_key,
    first_key,
    second_key,
    w_value,
    first_value,
    second_value,
    norm_train,
    norm_step,
):
    result_query = w_query - learn_rate * (
        first_query / (jnp.sqrt(second_query) + tiny_value) + decay_rate * w_query
    )
    result_key = w_key - learn_rate * (
        first_key / (jnp.sqrt(second_key) + tiny_value) + decay_rate * w_key
    )
    result_value = w_value - learn_rate * (
        first_value / (jnp.sqrt(second_value) + tiny_value) + decay_rate * w_value
    )
    total_query, total_key, total_value = lax.psum(
        (
            jnp.sum(jnp.abs(result_query), axis=0),
            jnp.sum(jnp.abs(result_key), axis=0),
            jnp.sum(jnp.abs(result_value), axis=0),
        ),
        "rows",
    )
    column_query = total_query / D_MODEL
    column_key = total_key / D_MODEL
    column_value = total_value / D_MODEL
    narrow_query, narrow_key, narrow_value = (
        (result_query / column_query).astype(jnp.bfloat16),
        (result_key / column_key).astype(jnp.bfloat16),
        (result_value / column_value).astype(jnp.bfloat16),
    )
    final_query, final_key, final_value = (
        lax.all_gather(narrow_query, "rows", axis=0, tiled=True),
        lax.all_gather(narrow_key, "rows", axis=0, tiled=True),
        lax.all_gather(narrow_value, "rows", axis=0, tiled=True),
    )
    serve_norm = lax.all_gather(
        (norm_train + norm_step).astype(jnp.bfloat16), ("rows", "model"), axis=0, tiled=True
    )
    return (
        final_query,
        final_key,
        final_value,
        column_query,
        column_key,
        column_value,
        serve_norm,
        result_query,
        result_key,
        result_value,
    )


def solution(mesh):
    placed = (
        P("rows", "model"),
        P("rows", "model"),
        P("rows", "model"),
        P("rows", "model"),
        P("rows", "model"),
        P("rows", "model"),
        P("rows", "model"),
        P("rows", "model"),
        P("rows", "model"),
        P(("rows", "model")),
        P(("rows", "model")),
    )
    return jax.shard_map(
        body,
        mesh=mesh,
        in_specs=placed,
        out_specs=(
            P(None, "model"),
            P(None, "model"),
            P(None, "model"),
            P("model"),
            P("model"),
            P("model"),
            P(),
            P("rows", "model"),
            P("rows", "model"),
            P("rows", "model"),
        ),
        check_vma=False,
    )
```

profile of v0, /device:TPU:0, one launch (start us, length us, event | category | flops | bytes accessed | tf_op | source)
XLA Modules:
  0.0 277.1 jit_solution(7815502317588367064)
XLA Ops:
  7.2 0.0 all-gather.7.cloned.1.call-start
  7.2 0.0 copy-start.5
  7.2 0.0 copy-start.6
  7.2 0.0 copy-start.7
  7.3 0.0 copy-start.8
  7.3 0.0 copy-start.9
  7.3 0.0 copy-start.10
  7.3 4.1 %abs_reduce_fusion = (f32[1024]{0:T(1024)S(1)}, f32[512,1024]{1,0:T(8,128)S(1)}) fusion(f32[512,1024]{1,0:T(8,128)} %param.11, f32[512,1024]{1,0:T(8,128)} %param.12, f32[512,1024]{1,0:T(8,128)} %param.13), kind=kLoop, calls=%fused_computation.1 | loop fusion | flops 4193280 | bytes 8392704 | tf_op jit(solution)/shard_map/reduce_sum | solution.py:38
  11.4 0.0 copy-done.5
  11.4 0.0 copy-done.6
  11.4 0.0 copy-done.7
  11.4 0.0 copy-done.8
  11.4 0.0 copy-done.9
  11.4 0.0 copy-done.10
  11.5 0.0 copy-start
  11.5 0.6 abs_reduce_fusion.1
  12.0 0.0 copy-start.3
  12.0 0.0 copy-start.4
  12.1 23.4 %all-reduce = (f32[1024]{0:T(1024)S(1)}, f32[256]{0:T(256)S(1)}, f32[256]{0:T(256)S(1)}) all-reduce(f32[1024]{0:T(1024)S(1)} %get-tuple-element.17, f32[256]{0:T(256)S(1)} %get-tuple-element.19, f32[256]{0:T(256)S(1)} %get-tuple-element.13), channel_id=1, replica_groups=mesh['rows'=8,'model'=4] {'rows'}, use_global_device_ids=true, to_apply=%region_1.0 | all-reduce | flops 1536 | bytes 12288 | tf_op jit(solution)/shard_map/psum | solution.py:36
  35.5 0.0 copy-start.12
  35.5 0.7 divide_convert_fusion.2
  36.2 0.0 all-gather.7.cloned.1.call-update
  36.3 0.0 all-gather.9.cloned.1.call-start
  36.3 0.0 copy-start.13
  36.3 0.7 divide_convert_fusion.1
  37.1 0.0 all-gather.9.cloned.1.call-update
  37.1 0.0 all-gather.5.cloned.1.call-start
  37.2 0.0 copy-start.11
  37.2 0.0 copy-done
  37.2 0.0 copy-start.14
  37.2 0.0 copy-start.15
  37.2 1.2 divide_convert_fusion
  38.4 0.0 copy-done.3
  38.4 0.0 copy-done.4
  38.4 0.0 copy-done.12
  38.4 0.0 copy-done.13
  38.4 0.0 all-gather.5.cloned.1.call-update
  38.5 0.0 copy-done.11
  38.5 0.0 copy-done.14
  38.5 0.0 copy-done.15
  38.5 38.2 %all-gather = bf16[32,1,128]{2,1,0:T(2,128)(2,1)S(1)} all-gather(bf16[1,1,128]{2,1,0:T(2,128)(2,1)S(1)} %convert_bitcast_fusion), channel_id=1, replica_groups=mesh['rows'=8,'model'=4] {'rows','model'}, dimensions={0}, use_global_device_ids=true | all-gather | bytes 8448 | tf_op jit(solution)/shard_map/all_gather | solution.py:57
  76.8 0.6 reduce
  77.4 5.5 %all-gather.7.cloned.1.call-done = bf16[4096,256]{1,0:T(8,128)(2,1)} async-done(((bf16[512,256]{1,0:T(8,128)(2,1)}), bf16[4096,256]{1,0:T(8,128)(2,1)}) %all-gather.7.cloned.1.call-update) | async-done | bytes 2097168 | tf_op jit(solution)/shard_map/all_gather | solution.py:54
  82.9 50.4 %all-gather.9.cloned.1.call-done = bf16[4096,256]{1,0:T(8,128)(2,1)} async-done(((bf16[512,256]{1,0:T(8,128)(2,1)}), bf16[4096,256]{1,0:T(8,128)(2,1)}) %all-gather.9.cloned.1.call-update) | async-done | bytes 2097168 | tf_op jit(solution)/shard_map/all_gather | solution.py:55
  133.3 125.7 %all-gather.5.cloned.1.call-done = bf16[4096,1024]{1,0:T(8,128)(2,1)} async-done(((bf16[512,1024]{1,0:T(8,128)(2,1)}), bf16[4096,1024]{1,0:T(8,128)(2,1)}) %all-gather.5.cloned.1.call-update) | async-done | bytes 8388624 | tf_op jit(solution)/shard_map/all_gather | solution.py:53
  259.0 0.0 copy-start.1
  259.0 7.9 %copy.24 = bf16[4096,1024]{1,0:T(8,128)(2,1)} copy(bf16[4096,1024]{1,0:T(8,128)(2,1)} %all-gather.5.cloned.1.call-done) | data formatting | bytes 16777216
  266.9 0.0 copy-done.1
  267.0 0.0 copy-start.2
  267.0 1.3 copy.25
  268.3 1.0 copy-done.2
  269.3 1.3 copy.26
  (4 shorter events, 0.0 us)
Async XLA Ops:
  7.2 75.7 %all-gather.7.cloned.1.call-start = ((), (), s32[]{:S(2)}) async-start(), calls=%async_computation.1 | async-start | bytes 2359296 | tf_op jit(solution)/shard_map/all_gather | solution.py:54
  7.2 4.2 %copy-start.5 = (f32[512,256]{1,0:T(8,128)S(1)}, f32[512,256]{1,0:T(8,128)}, u32[]{:S(2)}) copy-start(f32[512,256]{1,0:T(8,128)} %param.17) | copy-start | bytes 1572868
  7.2 4.2 %copy-start.6 = (f32[512,256]{1,0:T(8,128)S(1)}, f32[512,256]{1,0:T(8,128)}, u32[]{:S(2)}) copy-start(f32[512,256]{1,0:T(8,128)} %param.18) | copy-start | bytes 1572868
  7.2 4.2 %copy-start.7 = (f32[512,256]{1,0:T(8,128)S(1)}, f32[512,256]{1,0:T(8,128)}, u32[]{:S(2)}) copy-start(f32[512,256]{1,0:T(8,128)} %param.19) | copy-start | bytes 1572868
  7.3 4.2 %copy-start.8 = (f32[512,256]{1,0:T(8,128)S(1)}, f32[512,256]{1,0:T(8,128)}, u32[]{:S(2)}) copy-start(f32[512,256]{1,0:T(8,128)} %param.14) | copy-start | bytes 1572868
  7.3 4.2 %copy-start.9 = (f32[512,256]{1,0:T(8,128)S(1)}, f32[512,256]{1,0:T(8,128)}, u32[]{:S(2)}) copy-start(f32[512,256]{1,0:T(8,128)} %param.15) | copy-start | bytes 1572868
  7.3 4.2 %copy-start.10 = (f32[512,256]{1,0:T(8,128)S(1)}, f32[512,256]{1,0:T(8,128)}, u32[]{:S(2)}) copy-start(f32[512,256]{1,0:T(8,128)} %param.16) | copy-start | bytes 1572868
  11.5 25.7 %copy-start = (f32[512,1024]{1,0:T(8,128)}, f32[512,1024]{1,0:T(8,128)S(1)}, u32[]{:S(2)}) copy-start(f32[512,1024]{1,0:T(8,128)S(1)} %get-tuple-element.38) | copy-start | bytes 6291460
  12.0 26.4 %copy-start.3 = (f32[512,256]{1,0:T(8,128)}, f32[512,256]{1,0:T(8,128)S(1)}, u32[]{:S(2)}) copy-start(f32[512,256]{1,0:T(8,128)S(1)} %get-tuple-element.40) | copy-start | bytes 1572868
  12.0 26.4 %copy-start.4 = (f32[512,256]{1,0:T(8,128)}, f32[512,256]{1,0:T(8,128)S(1)}, u32[]{:S(2)}) copy-start(f32[512,256]{1,0:T(8,128)S(1)} %get-tuple-element.39) | copy-start | bytes 1572868
  35.5 3.0 %copy-start.12 = (f32[256]{0:T(256)}, f32[256]{0:T(256)S(1)}, u32[]{:S(2)}) copy-start(f32[256]{0:T(256)S(1)} %broadcast_multiply_fusion.2) | copy-start | bytes 3076
  36.3 97.0 %all-gather.9.cloned.1.call-start = ((), (), s32[]{:S(2)}) async-start(), calls=%async_computation.2 | async-start | bytes 2359296 | tf_op jit(solution)/shard_map/all_gather | solution.py:55
  36.3 2.1 copy-start.13
  37.1 221.9 %all-gather.5.cloned.1.call-start = ((), (), s32[]{:S(2)}) async-start(), calls=%async_computation | async-start | bytes 9437184 | tf_op jit(solution)/shard_map/all_gather | solution.py:53
  37.2 1.3 copy-start.11
  37.2 1.3 copy-start.14
  37.2 1.3 copy-start.15
  259.0 7.9 %copy-start.1 = (bf16[4096,256]{1,0:T(8,128)(2,1)S(1)}, bf16[4096,256]{1,0:T(8,128)(2,1)}, u32[]{:S(2)}) copy-start(bf16[4096,256]{1,0:T(8,128)(2,1)} %all-gather.7.cloned.1.call-done) | copy-start | bytes 6291460
  267.0 2.3 copy-start.2
Sparse Core Ops, SparseCore 0:
  36.4 46.5 all-gather.6
  85.6 47.6 all-gather.8
  136.0 122.9 all-gather.4
where the time goes:
time: 277 us
  waiting for transfers between devices  182 us (66%)
  blocking collectives  61.6 us (22%)
  between operations  14 us (5%)
  local copies, waits for them, and re-layouts  11.7 us (4%)
  other arithmetic  8.06 us (3%)
    all_gather x1, waiting for transfers between devices, body(): lax.all_gather(narrow_query, 'rows', axis=0, tiled=True)  126 us
    all_gather x1, waiting for transfers between devices, body(): lax.all_gather(narrow_value, 'rows', axis=0, tiled=True)  50.4 us
    all_gather x1, blocking collectives, body(): lax.all_gather((norm_train + norm_step).astype(jnp.bfloat16), ('rows', 'm...  38.2 us
    psum x1, blocking collectives, body(): lax.psum((jnp.sum(jnp.abs(result_query), axis=0), jnp.sum(jnp.abs(result_...  23.4 us
    unnamed x35, local copies, waits for them, and re-layouts  11.7 us
  transfers between devices with their start and end apart: 3, of which 3 were waited for; matrix products, arithmetic and copies ran while one was open for 1% of the time, Pallas kernels for 0%

commit v1 on v0

v1 whole, which is shorter than its diff:
```python
import functools

import jax
import jax.numpy as jnp
from jax import lax
from jax.experimental import pallas as pl
from jax.experimental.pallas import tpu as pltpu
from jax.sharding import PartitionSpec as P

learn_rate = 0.01
decay_rate = 0.05
tiny_value = 1e-08

MESH = pl.DeviceIdType.MESH
SIDE = 2
TILE = 32


def adam(w, first, second):
    return w - learn_rate * (first / (jnp.sqrt(second) + tiny_value) + decay_rate * w)


def plain(d_model, arrays):
    *weights, norm_train, norm_step = arrays
    results = [adam(*weights[3 * i : 3 * i + 3]) for i in range(3)]
    totals = lax.psum(tuple(jnp.sum(jnp.abs(r), axis=0) for r in results), "rows")
    columns = [t / d_model for t in totals]
    finals = [
        lax.all_gather((r / c).astype(jnp.bfloat16), "rows", axis=0, tiled=True)
        for r, c in zip(results, columns)
    ]
    serve = lax.all_gather(
        (norm_train + norm_step).astype(jnp.bfloat16), ("rows", "model"), axis=0, tiled=True
    )
    return (*finals, *columns, serve, *results)


def kernel(
    n_rows, n_model, blocks, d_model,
    *refs,
):
    ins, refs = refs[:9], refs[9:]
    nt_ref, ns_ref = refs[:2]
    finals, cols, norm_out, results = refs[2:5], refs[5:8], refs[8], refs[9:12]
    bufs = refs[12:21]
    (sums, gains, in_sem, sum_send, sum_recv, gain_send, gain_recv,
     up_send, down_send, side_send, line_recv, side_recv) = refs[21:]

    line = n_rows // SIDE
    me = lax.axis_index("rows")
    col = lax.axis_index("model")
    z, y = me // SIDE, me % SIDE
    other = 1 - y
    share = bufs[0].shape[0]
    nb = len(blocks)
    lead = nb - 1

    loads = []
    for b, (a, start, width) in enumerate(blocks):
        for k in range(3):
            where = (slice(None), pl.ds(start, width))
            c = pltpu.make_async_copy(
                ins[3 * a + k].at[where], bufs[3 * a + k].at[where], in_sem.at[b, k]
            )
            c.start()
            loads.append(c)

    barrier = pltpu.get_barrier_semaphore()
    for k in range(1, n_rows):
        pl.semaphore_signal(
            barrier, inc=1, device_id={"rows": lax.rem(me + k, n_rows)}, device_id_type=MESH
        )
    for k in range(1, n_model):
        pl.semaphore_signal(
            barrier, inc=1, device_id={"model": lax.rem(col + k, n_model)}, device_id_type=MESH
        )
    gains[me, col] = nt_ref[...] + ns_ref[...]

    def step(b):
        a, start, width = blocks[b]
        for k in range(3):
            loads[3 * b + k].wait()

        def one(i, acc):
            rows = pl.ds(pl.multiple_of(i * TILE, TILE), TILE)
            where = (rows, pl.ds(start, width))
            r = adam(*(bufs[3 * a + k][where] for k in range(3)))
            results[a][where] = r
            m = jnp.abs(r).reshape(TILE // 8, 8, width)
            return acc + jnp.sum(m, axis=0)

        acc = lax.fori_loop(0, share // TILE, one, jnp.zeros((8, width), jnp.float32))
        sums[b, me] = jnp.sum(acc, axis=0, keepdims=True)

    def sum_copy(b, k):
        return pltpu.make_async_remote_copy(
            src_ref=sums.at[b, me],
            dst_ref=sums.at[b, me],
            send_sem=sum_send.at[b, k],
            recv_sem=sum_recv.at[b, k],
            device_id={"rows": lax.rem(me + k, n_rows)},
            device_id_type=MESH,
        )

    def wait_sum(b, k):
        who = lax.rem(me + n_rows - k, n_rows)
        pltpu.make_async_remote_copy(
            src_ref=sums.at[b, who],
            dst_ref=sums.at[b, who],
            send_sem=sum_send.at[b, k],
            recv_sem=sum_recv.at[b, k],
            device_id={"rows": lax.rem(me + k, n_rows)},
            device_id_type=MESH,
        ).wait_recv()

    def place(j, owner):
        a, start, width = blocks[j]
        rows = pl.ds(pl.multiple_of(owner * share, share), share)
        return finals[a].at[rows, pl.ds(start, width)]

    def to_line(zs, j, up):
        owner = zs * SIDE + (other if j == nb else y)
        part = place(min(j, lead), owner)
        return pltpu.make_async_remote_copy(
            src_ref=part,
            dst_ref=part,
            send_sem=(up_send if up else down_send).at[zs, j],
            recv_sem=line_recv.at[zs, j],
            device_id={"rows": me + (SIDE if up else -SIDE)},
            device_id_type=MESH,
        )

    def to_side(zs, j, mine=True):
        part = place(j, zs * SIDE + (y if mine else other))
        return pltpu.make_async_remote_copy(
            src_ref=part,
            dst_ref=part,
            send_sem=side_send.at[zs, j],
            recv_sem=side_recv.at[zs, j],
            device_id={"rows": z * SIDE + other},
            device_id_type=MESH,
        )

    def both_ways(zs, j):
        @pl.when(z > 0)
        def _():
            to_line(zs, j, False).start()

        @pl.when(z < line - 1)
        def _():
            to_line(zs, j, True).start()

    def gain_model(k):
        return pltpu.make_async_remote_copy(
            src_ref=gains.at[me, col],
            dst_ref=gains.at[me, col],
            send_sem=gain_send.at[k],
            recv_sem=gain_recv.at[k],
            device_id={"model": lax.rem(col + k, n_model)},
            device_id_type=MESH,
        )

    def gain_rows(k, who):
        return pltpu.make_async_remote_copy(
            src_ref=gains.at[who],
            dst_ref=gains.at[who],
            send_sem=gain_send.at[n_model + k],
            recv_sem=gain_recv.at[n_model + k],
            device_id={"rows": lax.rem(me + k, n_rows)},
            device_id_type=MESH,
        )

    order = [0, lead] + list(range(1, lead))
    for i, b in enumerate(order):
        step(b)
        if i == 0:
            pl.semaphore_wait(barrier, n_rows + n_model - 2)
        for k in range(1, n_rows):
            sum_copy(b, k).start()
    for k in range(1, n_model):
        gain_model(k).start()

    for b in order:
        a, start, width = blocks[b]
        for k in range(1, n_rows):
            wait_sum(b, k)
        total = sums[b, 0]
        for k in range(1, n_rows):
            total = total + sums[b, k]
        column = total / d_model
        cols[a][:, pl.ds(start, width)] = column
        scale = jnp.broadcast_to(1.0 / column, (TILE, width))

        def one(i, carry):
            rows = pl.ds(pl.multiple_of(i * TILE, TILE), TILE)
            there = pl.ds(pl.multiple_of(me * share + i * TILE, TILE), TILE)
            where = pl.ds(start, width)
            finals[a][there, where] = (results[a][rows, where] * scale).astype(jnp.bfloat16)
            return carry

        lax.fori_loop(0, share // TILE, one, 0)
        if b != lead:
            both_ways(z, b)
        to_side(z, b).start()
    both_ways(z, lead)

    for k in range(1, n_model):
        who = lax.rem(col + n_model - k, n_model)
        pltpu.make_async_remote_copy(
            src_ref=gains.at[me, who],
            dst_ref=gains.at[me, who],
            send_sem=gain_send.at[k],
            recv_sem=gain_recv.at[k],
            device_id={"model": lax.rem(col + k, n_model)},
            device_id_type=MESH,
        ).wait_recv()
    for k in range(1, n_rows):
        gain_rows(k, me).start()

    to_side(z, lead, False).wait_recv()
    both_ways(z, nb)

    for d in range(1, line):
        for j in range(nb + 1):

            @pl.when(z - d >= 0)
            def _():
                to_line(z - d, j, True).wait_recv()

                @pl.when(z < line - 1)
                def _():
                    to_line(z - d, j, True).start()

                if j < lead:
                    to_side(z - d, j).start()

            @pl.when(z + d < line)
            def _():
                to_line(z + d, j, False).wait_recv()

                @pl.when(z > 0)
                def _():
                    to_line(z + d, j, False).start()

                if j < lead:
                    to_side(z + d, j).start()

    for k in range(1, n_rows):
        gain_rows(k, lax.rem(me + n_rows - k, n_rows)).wait_recv()
    norm_out[...] = gains[...]

    for zs in range(line):
        for j in range(lead):
            to_side(zs, j, False).wait_recv()
    for k in range(1, n_model):
        gain_model(k).wait_send()
    for k in range(1, n_rows):
        gain_rows(k, me).wait_send()
        for b in range(nb):
            sum_copy(b, k).wait_send()
    for zs in range(line):
        for j in range(lead):
            to_side(zs, j).wait_send()
        for j in range(nb + 1):

            @pl.when((z > 0) & (z <= zs))
            def _():
                to_line(zs, j, False).wait_send()

            @pl.when((z < line - 1) & (z >= zs))
            def _():
                to_line(zs, j, True).wait_send()
    to_side(z, lead).wait_send()


def fused(n_rows, n_model, d_model, blocks, arrays):
    *weights, norm_train, norm_step = arrays
    share = weights[0].shape[0]
    widths = [weights[3 * a].shape[1] for a in range(3)]
    line, nb = n_rows // SIDE, len(blocks)
    unit = norm_train.shape[0]
    anywhere = pl.BlockSpec(memory_space=pl.ANY)
    vmem = pl.BlockSpec(memory_space=pltpu.VMEM)
    f32, dma = jnp.float32, pltpu.SemaphoreType.DMA
    out = pl.pallas_call(
        functools.partial(kernel, n_rows, n_model, blocks, d_model),
        out_shape=[
            *(pltpu.VMEM((d_model, w), jnp.bfloat16) for w in widths),
            *(pltpu.VMEM((1, w), f32) for w in widths),
            pltpu.VMEM((n_rows, n_model, 1, unit), f32),
            *(pltpu.VMEM((share, w), f32) for w in widths),
        ],
        in_specs=[anywhere] * 9 + [vmem] * 2,
        out_specs=[vmem] * 10,
        scratch_shapes=[
            *(pltpu.VMEM((share, w), f32) for w in widths for _ in range(3)),
            pltpu.VMEM((nb, n_rows, 1, blocks[0][2]), f32),
            pltpu.VMEM((n_rows, n_model, 1, unit), f32),
            dma((nb, 3)),
            dma((nb, n_rows)),
            dma((nb, n_rows)),
            dma((n_rows + n_model,)),
            dma((n_rows + n_model,)),
            dma((line, nb + 1)),
            dma((line, nb + 1)),
            dma((line, nb)),
            dma((line, nb + 1)),
            dma((line, nb)),
        ],
        compiler_params=pltpu.CompilerParams(
            collective_id=0, has_side_effects=True, vmem_limit_bytes=48 * 2**20
        ),
    )(*weights, norm_train.reshape(1, -1), norm_step.reshape(1, -1))
    finals, cols, norm, results = out[:3], out[3:6], out[6], out[7:]
    serve = norm.reshape(-1).astype(jnp.bfloat16)
    return (*finals, *(c.reshape(-1) for c in cols), serve, *results)


def solution(mesh):
    n_rows, n_model = mesh.shape["rows"], mesh.shape["model"]

    def body(*arrays):
        share = arrays[0].shape[0]
        widths = [arrays[3 * a].shape[1] for a in range(3)]
        width = min(widths)
        d_model = share * n_rows
        fits = (
            n_rows % SIDE == 0
            and 2 <= n_rows // SIDE <= 4
            and share % TILE == 0
            and width % 128 == 0
            and all(w % width == 0 for w in widths)
        )
        if not fits:
            return plain(d_model, arrays)
        blocks = tuple(
            (a, s, width) for a, w in enumerate(widths) for s in range(0, w, width)
        )
        return fused(n_rows, n_model, d_model, blocks, arrays)

    return jax.shard_map(
        body,
        mesh=mesh,
        in_specs=(P("rows", "model"),) * 9 + (P(("rows", "model")),) * 2,
        out_specs=(
            *(P(None, "model"),) * 3,
            *(P("model"),) * 3,
            P(),
            *(P("rows", "model"),) * 3,
        ),
        check_vma=False,
    )
```

time: 277 us -> 144 us (0.52)
  waiting for transfers between devices: 182 us -> 0 us
  Pallas kernels: 0 us -> 132 us
  blocking collectives: 61.6 us -> 0 us
  between operations: 14 us -> 0.66 us
  other arithmetic: 8.06 us -> 0.65 us
    all_gather x3 -> x0, waiting for transfers between devices: 182 us -> none  [the longest x1 126 us: body(): lax.all_gather(narrow_query, 'rows', axis=0, tiled=True)]
    pallas_call x0 -> x1, Pallas kernels: none -> 132 us  [fused(): pl.pallas_call(functools.partial(kernel, n_rows, n_model, blocks, d_model...]
    all_gather x1 -> x0, blocking collectives: 38.2 us -> none  [body(): lax.all_gather((norm_train + norm_step).astype(jnp.bfloat16), ('rows', 'm...]
    psum x1 -> x0, blocking collectives: 23.4 us -> none  [body(): lax.psum((jnp.sum(jnp.abs(result_query), axis=0), jnp.sum(jnp.abs(result_...]
    reduce_sum x2 -> x0, other arithmetic: 4.68 us -> none  [the longest x1 4.11 us: body(): jnp.sum(jnp.abs(result_query), axis=0)]
    unnamed x35 -> x9, local copies, waits for them, and re-layouts: 11.7 us -> 10.7 us
  transfers between devices with their start and end apart: 3 -> 0, of which waited for: 3 -> 0; matrix products, arithmetic and copies ran while one was open for 1% -> 0% of each run, Pallas kernels for 0% -> 0%
where the time goes in v1:
time: 144 us
  Pallas kernels  132 us (92%)
  local copies, waits for them, and re-layouts  10.7 us (7%)
    pallas_call x1, Pallas kernels, fused(): pl.pallas_call(functools.partial(kernel, n_rows, n_model, blocks, d_model...  132 us
    unnamed x9, local copies, waits for them, and re-layouts  10.7 us

profile of v1, /device:TPU:0, one launch (start us, length us, event | category | flops | bytes accessed | tf_op | source)
XLA Modules:
  0.0 143.9 jit_solution(1575592376546579349)
XLA Ops:
  0.6 131.9 %shard_map.186 = (bf16[4096,1024]{1,0:T(8,128)(2,1)S(1)}, bf16[4096,256]{1,0:T(8,128)(2,1)S(1)}, bf16[4096,256]{1,0:T(8,128)(2,1)S(1)}, f32[1,1024]{1,0:T(1,128)...) custom-call(f32[512,1024]{1,0:T(8,128)} %refs_0_.1, ...), custom_call_target="tpu_custom_call" | custom-call | tf_op jit(solution)/shard_map/pallas_call | solution.py:285
  132.6 3.4 %copy.30 = bf16[4096,1024]{1,0:T(8,128)(2,1)} copy(bf16[4096,1024]{1,0:T(8,128)(2,1)S(1)} %get-tuple-element.30) | data formatting | bytes 16777216
  136.0 0.6 copy.34
  136.5 0.6 copy.35
  137.1 0.6 copy.33
  137.7 0.6 convert_reduce_fusion
  138.3 0.8 copy.37
  139.1 0.8 copy.38
  139.9 1.3 copy.31
  141.2 1.3 copy.32
  142.6 1.3 copy.36

commit v2 on v1

--- a/solution.py
+++ b/solution.py
@@ -14,6 +14,7 @@
 MESH = pl.DeviceIdType.MESH
 SIDE = 2
 TILE = 32
+PIECES = 4
 
 
 def adam(w, first, second):
@@ -247,7 +248,9 @@
 
     for k in range(1, n_rows):
         gain_rows(k, lax.rem(me + n_rows - k, n_rows)).wait_recv()
-    norm_out[...] = gains[...]
+    for r in range(n_rows):
+        for m in range(n_model):
+            norm_out[pl.ds(r * n_model + m, 1), :] = gains[r, m]
 
     for zs in range(line):
         for j in range(lead):
@@ -271,6 +274,19 @@
             def _():
                 to_line(zs, j, True).wait_send()
     to_side(z, lead).wait_send()
+
+
+def write(pieces, *refs):
+    ins, outs, sem = refs[:10], refs[10:20], refs[20]
+    copies = []
+    for n, (i, start, rows) in enumerate(pieces):
+        where = pl.ds(start, rows)
+        c = pltpu.make_async_copy(ins[i].at[where], outs[i].at[where], sem.at[n])
+        c.start()
+        copies.append(c)
+    outs[6][...] = ins[6][...].astype(jnp.bfloat16)
+    for c in copies:
+        c.wait()
 
 
 def fused(n_rows, n_model, d_model, blocks, arrays):
@@ -287,7 +303,7 @@
         out_shape=[
             *(pltpu.VMEM((d_model, w), jnp.bfloat16) for w in widths),
             *(pltpu.VMEM((1, w), f32) for w in widths),
-            pltpu.VMEM((n_rows, n_model, 1, unit), f32),
+            pltpu.VMEM((n_rows * n_model, unit), f32),
             *(pltpu.VMEM((share, w), f32) for w in widths),
         ],
         in_specs=[anywhere] * 9 + [vmem] * 2,
@@ -311,9 +327,23 @@
             collective_id=0, has_side_effects=True, vmem_limit_bytes=48 * 2**20
         ),
     )(*weights, norm_train.reshape(1, -1), norm_step.reshape(1, -1))
-    finals, cols, norm, results = out[:3], out[3:6], out[6], out[7:]
-    serve = norm.reshape(-1).astype(jnp.bfloat16)
-    return (*finals, *(c.reshape(-1) for c in cols), serve, *results)
+    pieces = []
+    for i in [0, 7, 1, 2, 8, 9, 3, 4, 5]:
+        rows = out[i].shape[0]
+        cut = rows // PIECES if i == 0 else rows
+        pieces += [(i, r, cut) for r in range(0, rows, cut)]
+    done = pl.pallas_call(
+        functools.partial(write, pieces),
+        out_shape=[
+            jax.ShapeDtypeStruct(o.shape, jnp.bfloat16 if i == 6 else o.dtype)
+            for i, o in enumerate(out)
+        ],
+        in_specs=[vmem if i == 6 else anywhere for i in range(10)],
+        out_specs=[vmem if i == 6 else anywhere for i in range(10)],
+        scratch_shapes=[dma((len(pieces),))],
+        compiler_params=pltpu.CompilerParams(vmem_limit_bytes=2**20),
+    )(*out)
+    return tuple(d.reshape(-1) if 3 <= i <= 6 else d for i, d in enumerate(done))
 
 
 def solution(mesh):

time: 144 us -> 139 us (0.965)
  local copies, waits for them, and re-layouts: 10.7 us -> 0 us
  Pallas kernels: 132 us -> 138 us
    unnamed x9 -> x0, local copies, waits for them, and re-layouts: 10.7 us -> none
    pallas_call x0 -> x1, Pallas kernels: none -> 6.2 us  [fused(): pl.pallas_call(functools.partial(write, pieces), out_shape=[jax.ShapeDtyp...]
where the time goes in v2:
time: 139 us
  Pallas kernels  138 us (99%)
    pallas_call x1, Pallas kernels, fused(): pl.pallas_call(functools.partial(kernel, n_rows, n_model, blocks, d_model...  132 us
    pallas_call x1, Pallas kernels, fused(): pl.pallas_call(functools.partial(write, pieces), out_shape=[jax.ShapeDtyp...  6.2 us

profile of v2, /device:TPU:0, one launch (start us, length us, event | category | flops | bytes accessed | tf_op | source)
XLA Modules:
  0.0 138.8 jit_solution(5352346169991653270)
XLA Ops:
  0.6 131.9 %shard_map.186 = (bf16[4096,1024]{1,0:T(8,128)(2,1)S(1)}, bf16[4096,256]{1,0:T(8,128)(2,1)S(1)}, bf16[4096,256]{1,0:T(8,128)(2,1)S(1)}, f32[1,1024]{1,0:T(1,128)...) custom-call(f32[512,1024]{1,0:T(8,128)} %refs_0_.1, ...), custom_call_target="tpu_custom_call" | custom-call | tf_op jit(solution)/shard_map/pallas_call | solution.py:301
  132.6 6.2 %shard_map.187 = (bf16[4096,1024]{1,0:T(8,128)(2,1)}, bf16[4096,256]{1,0:T(8,128)(2,1)}, bf16[4096,256]{1,0:T(8,128)(2,1)}, f32[1,1024]{1,0:T(1,128)}, f32[1,256...) custom-call(bf16[4096,1024]{1,0:T(8,128)(2,1)S(1)} %get-tuple-elemen, ...), custom_call_target="tpu_custom_call" | custom-call | tf_op jit(solution)/shard_map/pallas_call | solution.py:335
